TPU v7x, 256 devices: a whole 4x4x8 slice. The times are simulated.
256 devices in a mesh: energy: 4 (over z_lo), orb: 4 (over x), kpt: 16 (over z_hi, y, core).
Axes of the slice: x: 4, y: 4, z: 8 (z_hi: 2, z_lo: 4; z = z_hi * 4 + z_lo), core: 2. Of those that a mesh axis runs over, the one named last changes fastest.
Arguments:
- lesser: bfloat16 [2, 4, 16, 1, 512, 512], P(None, 'energy', 'kpt', None, None, 'orb'), may hold values from -6 to 6
- coupling: bfloat16 [2, 16, 512, 512], P(None, None, None, 'orb'), may hold values from -0.046875 to 0.046875
- transfer_map: int32 [16, 16], replicated, may hold values from 0 to 15, as said below
Outputs:
- sigma: bfloat16 [2, 4, 16, 1, 512, 512], P(None, None, 'kpt', None, 'energy', 'orb')
Inputs may be any that keep to these rules, and one draw needn't show every extreme that they name: transfer_map[k, p] is the index of the momentum transfer k - p: each row and each column holds every number of 0 to 15 once.
All inputs are finite; a program needn't handle non-finite values.
Results may differ from a plain program's by a relative error of at most 0.001.
Values may be sent and summed in bfloat16 or wider, within the bound.
A program may use at most 64 MiB of HBM per device.

v0:
```python
import jax
import jax.numpy as jnp
from jax import lax
from jax.sharding import Mesh
from jax.sharding import PartitionSpec as P

KPT = ("kpt_0", "kpt_1", "kpt_2")


def from_everyone(array, axis):
    peers = lax.axis_size(axis)
    return lax.all_to_all(
        jnp.broadcast_to(array[None], (peers, *array.shape)), axis, 0, 0, tiled=True
    )


def in_order(blocks, dim):
    shape = list(blocks.shape[1:])
    shape[dim] *= blocks.shape[0]
    return jnp.moveaxis(blocks, 0, dim).reshape(shape)


def gather_directly(array, axis, dim):
    blocks = from_everyone(array, axis)
    return in_order(blocks, dim)


def cut_along(array, dim, peers):
    shape = array.shape
    blocks = array.reshape(*shape[:dim], peers, shape[dim] // peers, *shape[dim + 1 :])
    return jnp.moveaxis(blocks, dim, 0)


def scatter_pairs(array, chips, core, dim):
    sizes = (lax.axis_size(chips), lax.axis_size(core))
    blocks = cut_along(array, dim, sizes[0] * sizes[1])
    inside = blocks.shape[1:]
    blocks = blocks.reshape(*sizes, *inside).swapaxes(0, 1).reshape(-1, *inside)
    blocks = lax.psum_scatter(blocks, core, scatter_dimension=0, tiled=True)
    return lax.psum_scatter(blocks, chips, scatter_dimension=0, tiled=True)[0]


def complex_terms(green, selected):
    real_out = jnp.einsum(
        "prm,tpmj->trj", green[0], selected[0], preferred_element_type=jnp.float32
    ) - jnp.einsum("prm,tpmj->trj", green[1], selected[1], preferred_element_type=jnp.float32)
    imag_out = jnp.einsum(
        "prm,tpmj->trj", green[0], selected[1], preferred_element_type=jnp.float32
    ) + jnp.einsum("prm,tpmj->trj", green[1], selected[0], preferred_element_type=jnp.float32)
    return (real_out, imag_out)


def per_device(lesser, coupling, transfer_map):
    regrouped = lax.all_to_all(lesser, "energy", split_axis=4, concat_axis=1, tiled=True)
    gathered = gather_directly(regrouped, "orb", 5)
    energies = gathered.shape[1]
    local_points = gathered.shape[2]
    layers = gathered.shape[3]
    tile = gathered.shape[4]
    width = gathered.shape[5]
    out_cols = coupling.shape[3]
    row_count = energies * layers * tile
    first_point = lax.axis_index(KPT) * local_points
    reordered = jnp.moveaxis(gathered, 2, 1).reshape(2, local_points, row_count, width)
    my_columns = lax.dynamic_slice_in_dim(transfer_map, first_point, local_points, 1)
    selected = jnp.take(coupling, my_columns, axis=1)
    real_out, imag_out = complex_terms(reordered, selected)
    mine = scatter_pairs(jnp.stack([real_out, imag_out], axis=1), ("kpt_0", "kpt_1"), "kpt_2", 0)
    summed = jnp.moveaxis(mine, 1, 0)
    result = summed.astype(jnp.bfloat16).reshape(2, local_points, energies, layers, tile, out_cols)
    return jnp.moveaxis(result, 1, 2)


def solution(mesh):
    split = Mesh(
        mesh.devices.reshape(mesh.shape["energy"], mesh.shape["orb"], 2, 4, 2),
        ("energy", "orb", "kpt_0", "kpt_1", "kpt_2"),
    )
    return jax.shard_map(
        per_device,
        mesh=split,
        in_specs=(P(None, "energy", KPT, None, None, "orb"), P(None, None, None, "orb"), P()),
        out_specs=P(None, None, KPT, None, "energy", "orb"),
        check_vma=False,
    )
```

profile of v0, /device:TPU:1, one launch (start us, length us, event | category | flops | bytes accessed | tf_op | source)
XLA Modules:
  0.0 243.9 jit_solution(6178791368518826517)
XLA Ops:
  6.5 0.0 copy-start.1
  6.5 1.2 copy.25
  7.8 13.1 %all_to_all.14 = bf16[2,1,1,1,512,128]{5,0,3,2,1,4:T(2,128)(2,1)S(1)} all-to-all(bf16[2,1,1,1,512,128]{5,0,3,2,1,4:T(2,128)(2,1)S(1)} %copy.25), channel_id=1, replica_groups=mesh['energy'=4,'orb'=4,'kpt_0'=2,'kpt_1'=4,'kpt_2'=2] {'energy'}, dimensions={4} | all-to-all | bytes 524288 | tf_op jit(solution)/shard_map/all_to_all | solution.py:54
  20.9 1.3 broadcast_in_dim.24
  22.2 4.0 %all-to-all-start.1 = ((bf16[4,2,4,1,1,128,128]{6,5,2,4,3,1,0:T(8,128)(2,1)}), bf16[4,2,4,1,1,128,128]{6,5,2,4,3,1,0:T(8,128)(2,1)S(1)}, u32[]{:S(2)}, u32[]{:S(2)}) async-start(bf16[4,2,4,1,1,128,128]{6,5,2,4,3,1,0:T(8,128)(2,1)} %broadcast_in_dim.24), calls=%async_computation.1 | async-start | bytes 2097152 | tf_op jit(solution)/shard_map/all_to_all | solution.py:12
  26.2 0.0 reduce-scatter.3.cloned.1.call-start
  26.2 0.0 copy-done.1
  26.2 0.2 fusion.2
  26.4 5.2 %gather_fusion = bf16[16,2,512,128]{3,2,1,0:T(8,128)(2,1)} fusion(bf16[2,16,512,128]{3,2,1,0:T(8,128)(2,1)} %param.4, s32[1024]{0:T(1024)S(1)} %pad_clamp_fusion), kind=kCustom, calls=%fused_computation | custom fusion | bytes 8388672 | tf_op jit(solution)/shard_map/jit(_take)/gather | solution.py:66
  31.6 6.2 %copy.24 = bf16[16,2,512,128]{2,3,0,1:T(8,128)(2,1)} copy(bf16[16,2,512,128]{3,2,1,0:T(8,128)(2,1)} %gather_fusion) | data formatting | bytes 8388608 | tf_op jit(solution)/shard_map/jit(_take)/gather | solution.py:66
  37.8 0.2 and_reduce_fusion
  38.0 4.6 %bitcast_select_fusion = bf16[2,16,1,512,128]{3,4,1,2,0:T(8,128)(2,1)} fusion(bf16[16,2,512,128]{2,3,0,1:T(8,128)(2,1)} %copy.24, pred[16]{0:T(512)(128)(4,1)S(1)} %and_reduce_fusion), kind=kLoop, calls=%fused_computation.2 | loop fusion | flops 2097152 | bytes 8388624 | tf_op jit(solution)/shard_map/jit(_take)/select_n | solution.py:66
  42.6 0.0 all-to-all-done.1
  42.6 0.1 fusion.3
  42.7 0.4 copy.27
  43.1 0.2 reshape.87
  43.4 0.0 copy-start
  43.4 5.0 %fusion.1 = f32[16,128,512]{2,1,0:T(8,128)} fusion(bf16[512,512,1]{1,0,2:T(8,128)(2,1)S(1)} %reshape.87, bf16[2,16,1,512,128]{3,4,1,2,0:T(8,128)(2,1)} %bitcast_select_fusion), kind=kOutput, calls=%fused_computation.8 | convolution fusion | flops 1073741824 | bytes 6815744 | tf_op jit(solution)/shard_map/prm,tpmj->trj/dot_general | solution.py:47
  48.4 0.0 copy-done
  48.4 3.2 %fusion = f32[16,128,512]{2,1,0:T(8,128)} fusion(bf16[512,512,1]{1,0,2:T(8,128)(2,1)S(1)} %reshape.87, bf16[2,16,1,512,128]{3,4,1,2,0:T(8,128)(2,1)S(1)} %copy-done), kind=kOutput, calls=%fused_computation.7 | convolution fusion | flops 1073741824 | bytes 6815744 | tf_op jit(solution)/shard_map/prm,tpmj->trj/dot_general | solution.py:44
  51.6 0.4 copy.28
  52.0 0.2 reshape.88
  52.2 6.1 %convolution_add_fusion = f32[16,128,512]{2,1,0:T(8,128)} fusion(f32[16,128,512]{2,1,0:T(8,128)} %fusion.1, bf16[512,512,1]{1,0,2:T(8,128)(2,1)S(1)} %reshape.88, bf16[2,16,1,512,128]{3,4,1,2,0:T(8,128)(2,1)} %bitcast_select_fusion), kind=kOutput, calls=%fused_computation.3 | convolution fusion | flops 1074790400 | bytes 11010048 | tf_op jit(solution)/shard_map/prm,tpmj->trj/dot_general | solution.py:49
  58.2 5.3 %copy.30 = f32[8,2,1,1,512,128]{5,4,3,0,1,2:T(8,128)} copy(f32[8,2,1,1,512,128]{4,5,1,0,3,2:T(8,128)} %bitcast.36) | data formatting | bytes 8388608 | tf_op jit(solution)/shard_map/stack | solution.py:68
  63.6 6.0 %convolution_subtract_fusion = f32[16,128,512]{2,1,0:T(8,128)} fusion(f32[16,128,512]{2,1,0:T(8,128)} %fusion, bf16[512,512,1]{1,0,2:T(8,128)(2,1)S(1)} %reshape.88, bf16[2,16,1,512,128]{3,4,1,2,0:T(8,128)(2,1)} %bitcast_select_fusion), kind=kOutput, calls=%fused_computation.4 | convolution fusion | flops 1074790400 | bytes 11010048 | tf_op jit(solution)/shard_map/prm,tpmj->trj/dot_general | solution.py:46
  69.6 5.3 %copy.29 = f32[8,2,1,1,512,128]{5,4,3,0,1,2:T(8,128)} copy(f32[8,2,1,1,512,128]{4,5,1,0,3,2:T(8,128)} %bitcast.35) | data formatting | bytes 8388608 | tf_op jit(solution)/shard_map/stack | solution.py:68
  75.0 7.6 %pad_maximum_fusion = f32[8,2,1,2,512,128]{5,4,3,0,1,2:T(8,128)} fusion(f32[8,2,1,1,512,128]{5,4,3,0,1,2:T(8,128)} %copy.30, f32[8,2,1,1,512,128]{5,4,3,0,1,2:T(8,128)} %copy.29), kind=kLoop, calls=%fused_computation.1 | loop fusion | flops 2097152 | bytes 16777216 | tf_op jit(solution)/shard_map/stack | solution.py:68
  82.6 0.0 reduce-scatter.3.cloned.1.call-update
  82.6 0.0 reduce-scatter.5.cloned.1.call-start
  82.6 25.9 %reduce-scatter.3.cloned.1.call-done = f32[8,1,2,512,128]{4,3,2,0,1:T(8,128)} async-done(((f32[16,1,2,512,128]{4,3,2,0,1:T(8,128)}), f32[8,1,2,512,128]{4,3,2,0,1:T(8,128)}) %reduce-scatter.3.cloned.1.call-update) | async-done | bytes 4194320 | tf_op jit(solution)/shard_map/reduce_scatter | solution.py:39
  108.5 0.0 reduce-scatter.5.cloned.1.call-update
  108.5 126.8 %reduce-scatter.5.cloned.1.call-done = f32[1,1,2,512,128]{4,3,2,0,1:T(8,128)} async-done(((f32[8,1,2,512,128]{4,3,2,0,1:T(8,128)}), f32[1,1,2,512,128]{4,3,2,0,1:T(8,128)}) %reduce-scatter.5.cloned.1.call-update) | async-done | bytes 524304 | tf_op jit(solution)/shard_map/reduce_scatter | solution.py:40
  235.3 1.8 convert_element_type.15
  (2 shorter events, 0.0 us)
Async XLA Ops:
  6.5 19.7 %copy-start.1 = (s32[16,16]{1,0:T(8,128)S(1)}, s32[16,16]{1,0:T(8,128)}, u32[]{:S(2)}) copy-start(s32[16,16]{1,0:T(8,128)} %param.5) | copy-start | bytes 3076
  22.2 20.4 %all-to-all-start.1 = ((bf16[4,2,4,1,1,128,128]{6,5,2,4,3,1,0:T(8,128)(2,1)}), bf16[4,2,4,1,1,128,128]{6,5,2,4,3,1,0:T(8,128)(2,1)S(1)}, u32[]{:S(2)}, u32[]{:S(2)}) async-start(bf16[4,2,4,1,1,128,128]{6,5,2,4,3,1,0:T(8,128)(2,1)} %broadcast_in_dim.24), calls=%async_computation.1 | async-start | bytes 2097152 | tf_op jit(solution)/shard_map/all_to_all | solution.py:12
  26.2 82.3 %reduce-scatter.3.cloned.1.call-start = ((), (), s32[]{:S(2)}) async-start(), calls=%async_computation.4 | async-start | bytes 12582912 | tf_op jit(solution)/shard_map/reduce_scatter | solution.py:39
  43.4 5.0 %copy-start = (bf16[2,16,1,512,128]{3,4,1,2,0:T(8,128)(2,1)S(1)}, bf16[2,16,1,512,128]{3,4,1,2,0:T(8,128)(2,1)}, u32[]{:S(2)}) copy-start(bf16[2,16,1,512,128]{3,4,1,2,0:T(8,128)(2,1)} %bitcast_select_fusion) | copy-start | bytes 12582916
  82.6 152.7 %reduce-scatter.5.cloned.1.call-start = ((), (), s32[]{:S(2)}) async-start(), calls=%async_computation.5 | async-start | bytes 4718592 | tf_op jit(solution)/shard_map/reduce_scatter | solution.py:40
Sparse Core Ops, SparseCore 0:
  82.7 25.7 reduce-scatter.2
  112.7 122.5 reduce-scatter.4
where the time goes:
time: 245 us; the launch traced here: 244 us
  waiting for transfers between devices  153 us (62%)
  local copies, waits for them, and re-layouts  26 us (11%)
  matrix products  20.3 us (8%)
  other arithmetic  14.4 us (6%)
  between operations  13.5 us (6%)
  blocking collectives  13.1 us (5%)
  starting transfers between devices  4.06 us (2%)
    reduce_scatter x1, waiting for transfers between devices, scatter_pairs(): return lax.psum_scatter(blocks, chips, scatter_dimension=0, tiled=True)[0]  127 us
    reduce_scatter x1, waiting for transfers between devices, scatter_pairs(): blocks = lax.psum_scatter(blocks, core, scatter_dimension=0, tiled=True)  25.9 us
    all_to_all x1, blocking collectives, per_device(): lax.all_to_all(lesser, 'energy', split_axis=4, concat_axis=1, tiled=True)  13.1 us
    gather x2, local copies, waits for them, and re-layouts, per_device(): selected = jnp.take(coupling, my_columns, axis=1)  11.4 us
    another operation x2, local copies, waits for them, and re-layouts, per_device(): jnp.stack([real_out, imag_out], axis=1)  10.7 us
    another operation x1, other arithmetic, per_device(): jnp.stack([real_out, imag_out], axis=1)  7.6 us
    dot_general x1, matrix products, complex_terms(): jnp.einsum('prm,tpmj->trj', green[1], selected[0], preferred_element_type...  6.07 us
    dot_general x1, matrix products, complex_terms(): jnp.einsum('prm,tpmj->trj', green[1], selected[1], preferred_element_type...  6.03 us
  transfers between devices with their start and end apart: 3, of which 2 were waited for; matrix products, arithmetic and copies ran while one was open for 7% of the time, Pallas kernels for 0%

commit v1 on v0

v1 whole, which is shorter than its diff:
```python
import jax
import jax.numpy as jnp
from jax import lax
from jax.experimental import pallas as pl
from jax.experimental.pallas import tpu as pltpu
from jax.sharding import PartitionSpec as P

MESH = pl.DeviceIdType.MESH
CHUNKS = 2
GROUPS = 4
NEAR_FIRST = (0, 1, 3, 2)


def kernel(lesser, coupling, table, out, src, green, u, y, packed, local_sem, u_sem,
           in_send, in_recv, x_send, x_recv, out_send, out_recv):
    slots = green.shape[2]
    rows = green.shape[4]
    per_group = slots // GROUPS
    z = lax.axis_index("energy")
    x = lax.axis_index("orb")
    k = lax.axis_index("kpt")
    z_hi, row, core = k // 8, (k // 2) % 4, k % 2
    right, left, opposite = (x + 1) % 4, (x + 3) % 4, (x + 2) % 4

    fetch = pltpu.make_async_copy(lesser, src, local_sem)
    fetch.start()
    fetch_u = pltpu.make_async_copy(coupling, u, u_sem)
    fetch_u.start()

    barrier = pltpu.get_barrier_semaphore()

    def greet(i, carry):
        pl.semaphore_signal(
            barrier, inc=1, device_id=((z + 1 + i // 16) % 4, x, (k + i) % 16), device_id_type=MESH
        )
        return carry

    for side in (left, right):
        pl.semaphore_signal(barrier, inc=1, device_id=(z, side, k), device_id_type=MESH)
    lax.fori_loop(0, 48, greet, 0)
    fetch.wait()
    pl.semaphore_wait(barrier, 50)

    def in_copy(chunk, core_to, near, z_hi_to):
        step = 2 * core_to + chunk
        tile = (z + 4 - step) % 4
        shift = 1 + 2 * (tile % 2) if step == 2 else 2
        row_to = (row + 4 - near) % 4
        part = z_hi_to * 4 + row_to
        slot = NEAR_FIRST.index(near) * 4 + z_hi * 2 + core
        begin = pl.multiple_of(tile * 128 + part * rows, rows)
        return pltpu.make_async_remote_copy(
            src_ref=src.at[:, pl.ds(begin, rows), :],
            dst_ref=green.at[chunk, x, slot],
            send_sem=in_send.at[chunk, (NEAR_FIRST.index(near) * 2 + z_hi_to) * 2 + core_to],
            recv_sem=in_recv.at[chunk, slot],
            device_id=((tile + shift) % 4, x, z_hi_to * 8 + row_to * 2 + core_to),
            device_id_type=MESH,
        )

    def all_in(act):
        for chunk in range(CHUNKS):
            for near in NEAR_FIRST:
                for z_hi_to in range(2):
                    for core_to in range(2):
                        act(in_copy(chunk, core_to, near, z_hi_to))

    all_in(lambda copy: copy.start())

    def x_copy(chunk, group, owner, to, lane):
        block = green.at[chunk, owner, pl.ds(group * per_group, per_group)]
        return pltpu.make_async_remote_copy(
            src_ref=block,
            dst_ref=block,
            send_sem=x_send.at[chunk, group, lane],
            recv_sem=x_recv.at[chunk, group, lane],
            device_id=(z, to, k),
            device_id_type=MESH,
        )

    def spread(chunk, group):
        for i in range(per_group):
            slot = group * per_group + i
            landed = green.at[chunk, x, slot]
            pltpu.make_async_remote_copy(
                src_ref=landed, dst_ref=landed, send_sem=in_send.at[chunk, slot],
                recv_sem=in_recv.at[chunk, slot], device_id=(z, right, k), device_id_type=MESH,
            ).wait_recv()
        x_copy(chunk, group, x, right, 0).start()
        x_copy(chunk, group, x, left, 1).start()

    def relay(chunk, group):
        x_copy(chunk, group, left, right, 0).wait_recv()
        if group % 2 == 0:
            x_copy(chunk, group, left, right, 2).start()
        x_copy(chunk, group, right, left, 1).wait_recv()
        if group % 2 == 1:
            x_copy(chunk, group, right, left, 2).start()

    def arrive(chunk, group):
        x_copy(chunk, group, opposite, right, 2).wait_recv()

    def product(chunk):
        def at(t, carry):
            lhs = jnp.concatenate(
                [green[chunk, m].reshape(slots * 2 * rows, 128) for m in range(4)], axis=1
            )
            rhs = jnp.concatenate([u[0, t], u[1, t]], axis=1)
            y[t] = jnp.dot(lhs, rhs, preferred_element_type=jnp.float32).reshape(y.shape[1:])
            return carry
        return at

    def combine(chunk):
        step = 2 * core + chunk
        shift = jnp.where(step == 2, 3 - 2 * (z % 2), 2)
        tile = (z + 4 - shift) % 4
        energy = (tile + step) % 4
        part = k // 2

        def out_copy(target):
            return pltpu.make_async_remote_copy(
                src_ref=packed.at[chunk, target],
                dst_ref=out.at[:, energy, pl.ds(pl.multiple_of(part * rows, rows), rows), :],
                send_sem=out_send.at[chunk, target],
                recv_sem=out_recv.at[energy, part],
                device_id=(tile, x, target),
                device_id_type=MESH,
            )

        def at(i, carry):
            target = (k + i) % 16
            real = jnp.zeros((rows, 128), jnp.float32)
            imag = jnp.zeros((rows, 128), jnp.float32)
            for slot in range(slots):
                near = NEAR_FIRST[slot // 4]
                point = (slot // 2) % 2 * 8 + (row + near) % 4 * 2 + slot % 2
                term = y[table[target, point], slot]
                real += term[0, :, :128] - term[1, :, 128:]
                imag += term[0, :, 128:] + term[1, :, :128]
            packed[chunk, target, 0] = real.astype(packed.dtype)
            packed[chunk, target, 1] = imag.astype(packed.dtype)
            out_copy(target).start()
            return carry

        return at, out_copy

    for group in range(GROUPS):
        spread(0, group)
    for group in range(GROUPS):
        relay(0, group)
        spread(1, group)
    for group in range(GROUPS):
        arrive(0, group)
    fetch_u.wait()
    lax.fori_loop(0, 16, product(0), 0)
    for group in range(GROUPS):
        relay(1, group)
    send0, out_copy0 = combine(0)
    lax.fori_loop(0, 16, send0, 0)
    for group in range(GROUPS):
        arrive(1, group)
    lax.fori_loop(0, 16, product(1), 0)
    send1, out_copy1 = combine(1)
    lax.fori_loop(0, 16, send1, 0)

    all_in(lambda copy: copy.wait_send())
    for chunk in range(CHUNKS):
        for group in range(GROUPS):
            for lane in range(3):
                x_copy(chunk, group, x, right, lane).wait_send()

    def settle(target, carry):
        out_copy0(target).wait_send()
        out_copy1(target).wait_send()
        return carry

    lax.fori_loop(0, 16, settle, 0)

    def collect(i, carry):
        energy, part = i // 8, i % 8
        landed = out.at[:, energy, pl.ds(pl.multiple_of(part * rows, rows), rows), :]
        pltpu.make_async_remote_copy(
            src_ref=packed.at[0, 0], dst_ref=landed, send_sem=out_send.at[0, 0],
            recv_sem=out_recv.at[energy, part], device_id=(z, right, k), device_id_type=MESH,
        ).wait_recv()
        return carry

    lax.fori_loop(0, 32, collect, 0)


def per_device(lesser, coupling, table):
    rows = 16
    result = pl.pallas_call(
        kernel,
        out_shape=jax.ShapeDtypeStruct((2, 4, 128, 128), jnp.bfloat16),
        in_specs=[
            pl.BlockSpec(memory_space=pl.ANY),
            pl.BlockSpec(memory_space=pl.ANY),
            pl.BlockSpec(memory_space=pltpu.SMEM),
        ],
        out_specs=pl.BlockSpec(memory_space=pltpu.VMEM),
        scratch_shapes=[
            pltpu.VMEM((2, 512, 128), jnp.bfloat16),
            pltpu.VMEM((CHUNKS, 4, 16, 2, rows, 128), jnp.bfloat16),
            pltpu.VMEM((2, 16, 512, 128), jnp.bfloat16),
            pltpu.VMEM((16, 16, 2, rows, 256), jnp.float32),
            pltpu.VMEM((CHUNKS, 16, 2, rows, 128), jnp.bfloat16),
            pltpu.SemaphoreType.DMA,
            pltpu.SemaphoreType.DMA,
            pltpu.SemaphoreType.DMA((CHUNKS, 16)),
            pltpu.SemaphoreType.DMA((CHUNKS, 16)),
            pltpu.SemaphoreType.DMA((CHUNKS, GROUPS, 3)),
            pltpu.SemaphoreType.DMA((CHUNKS, GROUPS, 3)),
            pltpu.SemaphoreType.DMA((CHUNKS, 16)),
            pltpu.SemaphoreType.DMA((4, 8)),
        ],
        compiler_params=pltpu.CompilerParams(collective_id=0, has_side_effects=True),
        name="convolve",
    )(lesser.reshape(2, 512, 128), coupling, table)
    return result.reshape(2, 4, 1, 1, 128, 128)


def solution(mesh):
    return jax.shard_map(
        per_device,
        mesh=mesh,
        in_specs=(P(None, "energy", "kpt", None, None, "orb"), P(None, None, None, "orb"), P()),
        out_specs=P(None, None, "kpt", None, "energy", "orb"),
        check_vma=False,
    )
```

time: 245 us -> 52 us (0.21)
  waiting for transfers between devices: 153 us -> 0 us
  Pallas kernels: 0 us -> 50.2 us
  local copies, waits for them, and re-layouts: 26 us -> 1.67 us
  matrix products: 20.3 us -> 0 us
  other arithmetic: 14.4 us -> 0 us
  between operations: 13.5 us -> 0.01 us
  blocking collectives: 13.1 us -> 0 us
  starting transfers between devices: 4.06 us -> 0 us
    reduce_scatter x2 -> x0, waiting for transfers between devices: 153 us -> none  [the longest x1 127 us: scatter_pairs(): return lax.psum_scatter(blocks, chips, scatter_dimension=0, tiled=True)[0]]
    pallas_call x0 -> x1, Pallas kernels: none -> 50.2 us  [per_device(): pl.pallas_call(kernel, out_shape=jax.ShapeDtypeStruct((2, 4, 128, 128), j...]
    dot_general x4 -> x0, matrix products: 20.3 us -> none  [the longest x1 6.07 us: complex_terms(): jnp.einsum('prm,tpmj->trj', green[1], selected[0], preferred_element_type...]
    all_to_all x1 -> x0, blocking collectives: 13.1 us -> none  [per_device(): lax.all_to_all(lesser, 'energy', split_axis=4, concat_axis=1, tiled=True)]
    gather x2 -> x0, local copies, waits for them, and re-layouts: 11.4 us -> none  [per_device(): selected = jnp.take(coupling, my_columns, axis=1)]
    another operation x4 -> x0, local copies, waits for them, and re-layouts: 11.1 us -> none  [the longest x2 10.7 us: per_device(): jnp.stack([real_out, imag_out], axis=1)]
    another operation x1 -> x0, other arithmetic: 7.6 us -> none  [per_device(): jnp.stack([real_out, imag_out], axis=1)]
    select_n x2 -> x0, other arithmetic: 4.81 us -> none  [per_device(): selected = jnp.take(coupling, my_columns, axis=1)]
  transfers between devices with their start and end apart: 3 -> 0, of which waited for: 2 -> 0; matrix products, arithmetic and copies ran while one was open for 7% -> 0% of each run, Pallas kernels for 0% -> 0%
where the time goes in v1:
time: 52 us; the launch traced here: 51.9 us
  Pallas kernels  50.2 us (97%)
  local copies, waits for them, and re-layouts  1.67 us (3%)
    pallas_call x1, Pallas kernels, per_device(): pl.pallas_call(kernel, out_shape=jax.ShapeDtypeStruct((2, 4, 128, 128), j...  50.2 us
    unnamed x1, local copies, waits for them, and re-layouts  1.67 us

profile of v1, /device:TPU:1, one launch (start us, length us, event | category | flops | bytes accessed | tf_op | source)
XLA Modules:
  0.0 51.9 jit_solution(3322175774522879231)
XLA Ops:
  0.0 50.2 %convolve.1 = bf16[2,4,128,128]{3,2,1,0:T(8,128)(2,1)} custom-call(bf16[2,512,128]{2,1,0:T(8,128)(2,1)} %bitcast.5, bf16[2,16,512,128]{3,2,1,0:T(8,128)(2,1)} %coupling.1, s32[16,16]{1,0:T(8,128)} %table.1), custom_call_target="tpu_custom_call" | custom-call | tf_op jit(solution)/shard_map/convolve/pallas_call | solution.py:193
  50.2 1.7 %copy.6 = bf16[2,4,1,1,128,128]{5,4,3,2,1,0:T(8,128)(2,1)} copy(bf16[2,4,1,1,128,128]{5,4,3,2,1,0:T(8,128)(2,1)} %bitcast.4) | data formatting | bytes 524288

commit v2 on v0

v2 whole, which is shorter than its diff:
```python
import contextlib
import itertools

import jax
import jax.numpy as jnp
from jax import lax
from jax.experimental import pallas as pl
from jax.experimental.pallas import tpu as pltpu
from jax.sharding import PartitionSpec as P

MESH = pl.DeviceIdType.MESH
scope = contextlib.nullcontext
CHUNKS = 2
GROUPS = 8
HALVES = 2
NEAR_FIRST = (0, 1, 3, 2)
X_STEPS = (0, 1, 3, 2)
DEAL = ((0, range(16)), (1, range(16)))
ORDER = (
    "S04", "S05", "S06", "A00", "U", "P00", "S07", "S14", "S15", "S16", "S17", "A10", "P10", "A01",
    "P01", "C0", "A11", "P11", "C1",
)


def kernel(lesser, coupling, table_in, out, src, green, u, y, packed, table, src_sem, u_sem, table_sem, own_sem,
           in_send, near_recv, in_recv, x_send, x_recv, out_send, out_recv):
    slots = green.shape[2]
    rows = green.shape[4]
    per_group = slots // GROUPS
    per_half = slots // HALVES
    z = lax.axis_index("energy")
    x = lax.axis_index("orb")
    k = lax.axis_index("kpt")
    z_hi, row, core = k // 8, (k // 2) % 4, k % 2

    fetch = pltpu.make_async_copy(lesser, src, src_sem)
    fetch.start()
    fetch_u = pltpu.make_async_copy(coupling, u, u_sem)
    fetch_u.start()
    own = []
    for chunk in range(CHUNKS):
        begin = pl.multiple_of((z + 4 - 2 * core - chunk) % 4 * 128 + k // 2 * rows, rows)
        own.append(
            pltpu.make_async_copy(
                lesser.at[:, pl.ds(begin, rows), :], green.at[chunk, x, 0], own_sem.at[chunk]
            )
        )
        own[-1].start()
    fetch_table = pltpu.make_async_copy(table_in, table, table_sem)
    fetch_table.start()

    def fetched():
        fetch_u.wait()
        fetch_table.wait()

    barrier = pltpu.get_barrier_semaphore()

    def greet(z_to, x_to, k_to):
        pl.semaphore_signal(barrier, inc=1, device_id=(z_to, x_to, k_to), device_id_type=MESH)

    def greet_near(i, carry):
        other = (x * 8 + k % 8 + i) % 32
        greet(z, other // 8, z_hi * 8 + other % 8)
        return carry

    def greet_far(i, carry):
        greet(z, x, (k + 8) // 8 % 2 * 8 + i)
        greet((z + 1) % 4, x, 2 * i)
        greet((z + 2) % 4, x, 2 * i + 1)
        greet((z + 3) % 4, x, 2 * i + 1)
        return carry

    lax.fori_loop(1, 32, greet_near, 0)
    lax.fori_loop(0, 8, greet_far, 0)
    with scope("s_fetch"):
        fetch.wait()
    with scope("s_barrier"):
        pl.semaphore_wait(barrier, 55 + 16 * core)

    def send(source, target, send_sem, recv_sem, place):
        return pltpu.make_async_remote_copy(
            src_ref=source, dst_ref=target, send_sem=send_sem, recv_sem=recv_sem,
            device_id=place, device_id_type=MESH,
        )

    def landed(block, recv_sem):
        send(block, block, x_send, recv_sem, (z, (x + 1) % 4, k)).wait_recv()

    def sent(block, send_sem):
        send(block, block, send_sem, out_recv, (z, (x + 1) % 4, k)).wait_send()

    places = tuple(itertools.product(range(2), NEAR_FIRST, range(2)))

    def deal(chunk, slot, x_step):
        z_step, near, core_step = places[slot]
        z_hi_to, row_to, core_to = (z_hi + z_step) % 2, (row + 4 - near) % 4, (core + core_step) % 2
        tile = (z + 4 - 2 * core_to - chunk) % 4
        begin = pl.multiple_of(tile * 128 + (z_hi_to * 4 + row_to) * rows, rows)
        send(
            src.at[:, pl.ds(begin, rows), :],
            green.at[chunk, x, slot],
            in_send,
            in_recv.at[chunk, slot // per_group] if z_step else near_recv.at[chunk],
            (z, (x + x_step) % 4, z_hi_to * 8 + row_to * 2 + core_to),
        ).start()

    for chunk, slots_of in DEAL:
        for slot in slots_of:
            for x_step in (0,) if slot >= per_half else X_STEPS:
                if (slot, x_step) != (0, 0):
                    deal(chunk, slot, x_step)

    def spread(chunk, group):
        block = green.at[chunk, x, pl.ds(group * per_group, per_group)]
        landed(block, in_recv.at[chunk, group])
        for x_step in X_STEPS[1:]:
            send(block, block, x_send, x_recv.at[chunk], (z, (x + x_step) % 4, k)).start()

    def arrive(chunk, half):
        if half:
            landed(green.at[chunk, pl.ds(0, 3), pl.ds(0, per_half)], x_recv.at[chunk])
        else:
            own[chunk].wait()
            landed(packed.at[pl.ds(0, 31)], near_recv.at[chunk])

    def product(chunk, half, extra=None):
        part = pl.ds(half * per_half, per_half)

        def at(t, carry):
            lhs = jnp.concatenate(
                [green[chunk, m, part].reshape(per_half * 2 * rows, 128) for m in range(4)], axis=1
            )
            rhs = jnp.concatenate([u[0, t], u[1, t]], axis=1)
            terms = jnp.dot(lhs, rhs, preferred_element_type=jnp.float32)
            y[chunk, t, part] = terms.reshape(per_half, 2, rows, 256)
            if extra is not None:
                total(extra, t)
            return carry

        lax.fori_loop(0, 16, at, 0, unroll=True)

    def target_of(i):
        far = jnp.where(i < 8, 2 + i // 4, 3 - i // 4)
        return (z_hi + 1 + i // 2) % 2 * 8 + (row + far) % 4 * 2 + (core + 1 + i) % 2

    def total(chunk, i):
        target = target_of(i)
        real = jnp.zeros((rows, 128), jnp.float32)
        imag = jnp.zeros((rows, 128), jnp.float32)
        for slot in range(slots):
            z_step, near, core_step = places[slot]
            point = (z_hi + z_step) % 2 * 8 + (row + near) % 4 * 2 + (core + core_step) % 2
            term = y[chunk, table[target, point], slot]
            real += term[0, :, :128] - term[1, :, 128:]
            imag += term[0, :, 128:] + term[1, :, :128]
        packed[chunk * 16 + i, 0] = real.astype(packed.dtype)
        packed[chunk * 16 + i, 1] = imag.astype(packed.dtype)

    def give(chunk, i):
        tile = (z + 4 - 2 * core - chunk) % 4
        begin = pl.ds(pl.multiple_of(k // 2 * rows, rows), rows)

        def away():
            send(
                packed.at[chunk * 16 + i], out.at[:, z, begin, :], out_send, out_recv,
                (tile, x, target_of(i)),
            ).start()

        if chunk > 0:
            away()
        else:
            stays = jnp.logical_and(core == 0, i == 15)
            pl.when(jnp.logical_not(stays))(away)

            @pl.when(stays)
            def _():
                out[:, z, begin, :] = packed[15]

    def combine(chunk):
        def at(i, carry):
            total(chunk, i)
            give(chunk, i)
            return carry

        lax.fori_loop(0, 16, at, 0)

    def give_all(chunk):
        def at(i, carry):
            give(chunk, i)
            return carry

        lax.fori_loop(0, 16, at, 0)

    def product_and_total(chunk, half):
        product(chunk, half, chunk - 1)

    act = {
        "S": spread, "A": arrive, "P": product, "C": combine, "U": fetched, "F": product_and_total, "G": give_all,
    }
    for name in ORDER:
        with scope("s_" + name):
            act[name[0]](*(int(digit) for digit in name[1:]))

    with scope("s_drain"):
        sent(green.at[:, pl.ds(0, 3), pl.ds(0, 13)], in_send)
        sent(green.at[:, pl.ds(0, 3), pl.ds(0, per_half)], x_send)
        for count in (31, 32):

            @pl.when(core == count - 31)
            def _():
                sent(packed.at[pl.ds(0, count)], out_send)
    with scope("s_collect"):
        for count in (31, 32):

            @pl.when(core == count - 31)
            def _():
                landed(packed.at[pl.ds(0, count)], out_recv)


def per_device(lesser, coupling, table):
    rows = 16
    result = pl.pallas_call(
        kernel,
        out_shape=pltpu.VMEM((2, 4, 128, 128), jnp.bfloat16),
        in_specs=[
            pl.BlockSpec(memory_space=pl.ANY),
            pl.BlockSpec(memory_space=pl.ANY),
            pl.BlockSpec(memory_space=pl.ANY),
        ],
        out_specs=pl.BlockSpec(memory_space=pltpu.VMEM),
        scratch_shapes=[
            pltpu.VMEM((2, 512, 128), jnp.bfloat16),
            pltpu.VMEM((CHUNKS, 4, 16, 2, rows, 128), jnp.bfloat16),
            pltpu.VMEM((2, 16, 512, 128), jnp.bfloat16),
            pltpu.VMEM((CHUNKS, 16, 16, 2, rows, 256), jnp.float32),
            pltpu.VMEM((CHUNKS * 16, 2, rows, 128), jnp.bfloat16),
            pltpu.SMEM((16, 16), jnp.int32),
            pltpu.SemaphoreType.DMA,
            pltpu.SemaphoreType.DMA,
            pltpu.SemaphoreType.DMA,
            pltpu.SemaphoreType.DMA((CHUNKS,)),
            pltpu.SemaphoreType.DMA,
            pltpu.SemaphoreType.DMA((CHUNKS,)),
            pltpu.SemaphoreType.DMA((CHUNKS, GROUPS)),
            pltpu.SemaphoreType.DMA,
            pltpu.SemaphoreType.DMA((CHUNKS,)),
            pltpu.SemaphoreType.DMA,
            pltpu.SemaphoreType.DMA,
        ],
        compiler_params=pltpu.CompilerParams(collective_id=0, has_side_effects=True),
        name="convolve",
    )(lesser.reshape(2, 512, 128), coupling, table)
    return result.reshape(2, 4, 1, 1, 128, 128)


def solution(mesh):
    return jax.shard_map(
        per_device,
        mesh=mesh,
        in_specs=(P(None, "energy", "kpt", None, None, "orb"), P(None, None, None, "orb"), P()),
        out_specs=P(None, None, "kpt", None, "energy", "orb"),
        check_vma=False,
    )
```

time: 245 us -> 36.8 us (0.15)
  waiting for transfers between devices: 153 us -> 0 us
  Pallas kernels: 0 us -> 36 us
  local copies, waits for them, and re-layouts: 26 us -> 0.71 us
  matrix products: 20.3 us -> 0 us
  other arithmetic: 14.4 us -> 0 us
  between operations: 13.5 us -> 0.01 us
  blocking collectives: 13.1 us -> 0 us
  starting transfers between devices: 4.06 us -> 0 us
    reduce_scatter x2 -> x0, waiting for transfers between devices: 153 us -> none  [the longest x1 127 us: scatter_pairs(): return lax.psum_scatter(blocks, chips, scatter_dimension=0, tiled=True)[0]]
    pallas_call x0 -> x1, Pallas kernels: none -> 36 us  [per_device(): pl.pallas_call(kernel, out_shape=pltpu.VMEM((2, 4, 128, 128), jnp.bfloat1...]
    dot_general x4 -> x0, matrix products: 20.3 us -> none  [the longest x1 6.07 us: complex_terms(): jnp.einsum('prm,tpmj->trj', green[1], selected[0], preferred_element_type...]
    all_to_all x1 -> x0, blocking collectives: 13.1 us -> none  [per_device(): lax.all_to_all(lesser, 'energy', split_axis=4, concat_axis=1, tiled=True)]
    gather x2 -> x0, local copies, waits for them, and re-layouts: 11.4 us -> none  [per_device(): selected = jnp.take(coupling, my_columns, axis=1)]
    another operation x4 -> x0, local copies, waits for them, and re-layouts: 11.1 us -> none  [the longest x2 10.7 us: per_device(): jnp.stack([real_out, imag_out], axis=1)]
    another operation x1 -> x0, other arithmetic: 7.6 us -> none  [per_device(): jnp.stack([real_out, imag_out], axis=1)]
    select_n x2 -> x0, other arithmetic: 4.81 us -> none  [per_device(): selected = jnp.take(coupling, my_columns, axis=1)]
  transfers between devices with their start and end apart: 3 -> 0, of which waited for: 2 -> 0; matrix products, arithmetic and copies ran while one was open for 7% -> 0% of each run, Pallas kernels for 0% -> 0%
where the time goes in v2:
time: 36.8 us; the launch traced here: 36.7 us
  Pallas kernels  36 us (98%)
  local copies, waits for them, and re-layouts  0.71 us (2%)
    pallas_call x1, Pallas kernels, per_device(): pl.pallas_call(kernel, out_shape=pltpu.VMEM((2, 4, 128, 128), jnp.bfloat1...  36 us

profile of v2, /device:TPU:1, one launch (start us, length us, event | category | flops | bytes accessed | tf_op | source)
XLA Modules:
  0.0 36.7 jit_solution(16994693180592125925)
XLA Ops:
  0.0 36.0 %convolve.1 = bf16[2,4,128,128]{3,2,1,0:T(8,128)(2,1)S(1)} custom-call(bf16[2,512,128]{2,1,0:T(8,128)(2,1)} %bitcast.5, bf16[2,16,512,128]{3,2,1,0:T(8,128)(2,1)} %coupling.1, s32[16,16]{1,0:T(8,128)} %table_in.1), custom_call_target="tpu_custom_call" | custom-call | tf_op jit(solution)/shard_map/convolve/pallas_call | solution.py:222
  36.0 0.7 %copy.6 = bf16[2,4,1,1,128,128]{5,4,3,2,1,0:T(8,128)(2,1)} copy(bf16[2,4,1,1,128,128]{5,4,3,2,1,0:T(8,128)(2,1)S(1)} %bitcast.4) | data formatting | bytes 524288

commit v3 on v2

--- a/solution.py
+++ b/solution.py
@@ -15,10 +15,11 @@
 HALVES = 2
 NEAR_FIRST = (0, 1, 3, 2)
 X_STEPS = (0, 1, 3, 2)
+FLIGHT = 1
 DEAL = ((0, range(16)), (1, range(16)))
 ORDER = (
-    "S04", "S05", "S06", "A00", "U", "P00", "S07", "S14", "S15", "S16", "S17", "A10", "P10", "A01",
-    "P01", "C0", "A11", "P11", "C1",
+    "S01", "S02", "S03", "S11", "S12", "S13", "S04", "S05", "S06", "S07", "A00", "U", "P00", "S14",
+    "S15", "S16", "S17", "A10", "P10", "A01", "P01", "C0", "A11", "P11", "C1",
 )
 
 
@@ -70,8 +71,8 @@
         greet((z + 3) % 4, x, 2 * i + 1)
         return carry
 
-    lax.fori_loop(1, 32, greet_near, 0)
-    lax.fori_loop(0, 8, greet_far, 0)
+    lax.fori_loop(0, 8, greet_far, 0, unroll=True)
+    lax.fori_loop(1, 32, greet_near, 0, unroll=True)
     with scope("s_fetch"):
         fetch.wait()
     with scope("s_barrier"):
@@ -100,13 +101,13 @@
             src.at[:, pl.ds(begin, rows), :],
             green.at[chunk, x, slot],
             in_send,
-            in_recv.at[chunk, slot // per_group] if z_step else near_recv.at[chunk],
+            near_recv.at[chunk] if slot < FLIGHT * per_group else in_recv.at[chunk, slot // per_group],
             (z, (x + x_step) % 4, z_hi_to * 8 + row_to * 2 + core_to),
         ).start()
 
     for chunk, slots_of in DEAL:
         for slot in slots_of:
-            for x_step in (0,) if slot >= per_half else X_STEPS:
+            for x_step in X_STEPS if slot < FLIGHT * per_group else (0,):
                 if (slot, x_step) != (0, 0):
                     deal(chunk, slot, x_step)
 
@@ -114,14 +115,16 @@
         block = green.at[chunk, x, pl.ds(group * per_group, per_group)]
         landed(block, in_recv.at[chunk, group])
         for x_step in X_STEPS[1:]:
-            send(block, block, x_send, x_recv.at[chunk], (z, (x + x_step) % 4, k)).start()
+            send(block, block, x_send, x_recv.at[chunk, group * HALVES // GROUPS], (z, (x + x_step) % 4, k)).start()
 
     def arrive(chunk, half):
-        if half:
-            landed(green.at[chunk, pl.ds(0, 3), pl.ds(0, per_half)], x_recv.at[chunk])
-        else:
+        spreads = GROUPS // HALVES
+        if half == 0:
             own[chunk].wait()
-            landed(packed.at[pl.ds(0, 31)], near_recv.at[chunk])
+            landed(packed.at[pl.ds(0, 4 * per_group * FLIGHT - 1)], near_recv.at[chunk])
+            spreads -= FLIGHT
+        if spreads:
+            landed(packed.at[pl.ds(0, 3 * per_group * spreads)], x_recv.at[chunk, half])
 
     def product(chunk, half, extra=None):
         part = pl.ds(half * per_half, per_half)
@@ -139,12 +142,17 @@
 
         lax.fori_loop(0, 16, at, 0, unroll=True)
 
-    def target_of(i):
-        far = jnp.where(i < 8, 2 + i // 4, 3 - i // 4)
-        return (z_hi + 1 + i // 2) % 2 * 8 + (row + far) % 4 * 2 + (core + 1 + i) % 2
+    wraps = z == 3 * core
+
+    def target_of(chunk, i):
+        far = jnp.where(i % 8 < 4, 2 + i % 8 // 2, 3 - i % 8 // 2)
+        z_step = 1 - i // 8
+        if chunk:
+            z_step = jnp.where(wraps, i // 8, z_step)
+        return (z_hi + z_step) % 2 * 8 + (row + far) % 4 * 2 + (core + 1 + i) % 2
 
     def total(chunk, i):
-        target = target_of(i)
+        target = target_of(chunk, i)
         real = jnp.zeros((rows, 128), jnp.float32)
         imag = jnp.zeros((rows, 128), jnp.float32)
         for slot in range(slots):
@@ -163,7 +171,7 @@
         def away():
             send(
                 packed.at[chunk * 16 + i], out.at[:, z, begin, :], out_send, out_recv,
-                (tile, x, target_of(i)),
+                (tile, x, target_of(chunk, i)),
             ).start()
 
         if chunk > 0:
@@ -202,8 +210,8 @@
             act[name[0]](*(int(digit) for digit in name[1:]))
 
     with scope("s_drain"):
-        sent(green.at[:, pl.ds(0, 3), pl.ds(0, 13)], in_send)
-        sent(green.at[:, pl.ds(0, 3), pl.ds(0, per_half)], x_send)
+        sent(u.at[:, pl.ds(0, 3), pl.ds(0, 160 + 64 * FLIGHT), :], in_send)
+        sent(u.at[:, pl.ds(0, 4), pl.ds(0, 384 - 48 * FLIGHT), :], x_send)
         for count in (31, 32):
 
             @pl.when(core == count - 31)
@@ -243,7 +251,7 @@
             pltpu.SemaphoreType.DMA((CHUNKS,)),
             pltpu.SemaphoreType.DMA((CHUNKS, GROUPS)),
             pltpu.SemaphoreType.DMA,
-            pltpu.SemaphoreType.DMA((CHUNKS,)),
+            pltpu.SemaphoreType.DMA((CHUNKS, HALVES)),
             pltpu.SemaphoreType.DMA,
             pltpu.SemaphoreType.DMA,
         ],

time: 36.8 us -> 36 us (0.978)
  Pallas kernels: 36 us -> 35.3 us
    pallas_call x1, Pallas kernels: 36 us -> 35.3 us  [per_device(): pl.pallas_call(kernel, out_shape=pltpu.VMEM((2, 4, 128, 128), jnp.bfloat1...]
where the time goes in v3:
time: 36 us
  Pallas kernels  35.3 us (98%)
  local copies, waits for them, and re-layouts  0.71 us (2%)
    pallas_call x1, Pallas kernels, per_device(): pl.pallas_call(kernel, out_shape=pltpu.VMEM((2, 4, 128, 128), jnp.bfloat1...  35.3 us

profile of v3, /device:TPU:1, one launch (start us, length us, event | category | flops | bytes accessed | tf_op | source)
XLA Modules:
  0.0 36.0 jit_solution(8375489534038055940)
XLA Ops:
  0.0 35.3 %convolve.1 = bf16[2,4,128,128]{3,2,1,0:T(8,128)(2,1)S(1)} custom-call(bf16[2,512,128]{2,1,0:T(8,128)(2,1)} %bitcast.5, bf16[2,16,512,128]{3,2,1,0:T(8,128)(2,1)} %coupling.1, s32[16,16]{1,0:T(8,128)} %table_in.1), custom_call_target="tpu_custom_call" | custom-call | tf_op jit(solution)/shard_map/convolve/pallas_call | solution.py:230
  35.3 0.7 %copy.6 = bf16[2,4,1,1,128,128]{5,4,3,2,1,0:T(8,128)(2,1)} copy(bf16[2,4,1,1,128,128]{5,4,3,2,1,0:T(8,128)(2,1)S(1)} %bitcast.4) | data formatting | bytes 524288

commit v4 on v3

--- a/solution.py
+++ b/solution.py
@@ -18,8 +18,9 @@
 FLIGHT = 1
 DEAL = ((0, range(16)), (1, range(16)))
 ORDER = (
-    "S01", "S02", "S03", "S11", "S12", "S13", "S04", "S05", "S06", "S07", "A00", "U", "P00", "S14",
-    "S15", "S16", "S17", "A10", "P10", "A01", "P01", "C0", "A11", "P11", "C1",
+    "S01", "S02", "S03", "S11", "S12", "S04", "S13", "S05", "S06", "S07", "A002", "U", "P002", "S14",
+    "S15", "S16", "S17", "A102", "P102", "A023", "P023", "A034", "P034", "C0", "A123", "P123", "A134",
+    "P134", "C1",
 )
 
 
@@ -115,29 +116,27 @@
         block = green.at[chunk, x, pl.ds(group * per_group, per_group)]
         landed(block, in_recv.at[chunk, group])
         for x_step in X_STEPS[1:]:
-            send(block, block, x_send, x_recv.at[chunk, group * HALVES // GROUPS], (z, (x + x_step) % 4, k)).start()
-
-    def arrive(chunk, half):
-        spreads = GROUPS // HALVES
-        if half == 0:
+            send(block, block, x_send, x_recv.at[chunk, group * 4 // GROUPS], (z, (x + x_step) % 4, k)).start()
+
+    def arrive(chunk, first, last):
+        if first == 0:
             own[chunk].wait()
             landed(packed.at[pl.ds(0, 4 * per_group * FLIGHT - 1)], near_recv.at[chunk])
-            spreads -= FLIGHT
-        if spreads:
-            landed(packed.at[pl.ds(0, 3 * per_group * spreads)], x_recv.at[chunk, half])
-
-    def product(chunk, half, extra=None):
-        part = pl.ds(half * per_half, per_half)
+        for quarter in range(first, last):
+            spreads = GROUPS // 4 - (FLIGHT if quarter == 0 else 0)
+            landed(packed.at[pl.ds(0, 3 * per_group * spreads)], x_recv.at[chunk, quarter])
+
+    def product(chunk, first, last):
+        count = slots // 4 * (last - first)
+        part = pl.ds(slots // 4 * first, count)
 
         def at(t, carry):
             lhs = jnp.concatenate(
-                [green[chunk, m, part].reshape(per_half * 2 * rows, 128) for m in range(4)], axis=1
+                [green[chunk, m, part].reshape(count * 2 * rows, 128) for m in range(4)], axis=1
             )
             rhs = jnp.concatenate([u[0, t], u[1, t]], axis=1)
             terms = jnp.dot(lhs, rhs, preferred_element_type=jnp.float32)
-            y[chunk, t, part] = terms.reshape(per_half, 2, rows, 256)
-            if extra is not None:
-                total(extra, t)
+            y[chunk, t, part] = terms.reshape(count, 2, rows, 256)
             return carry
 
         lax.fori_loop(0, 16, at, 0, unroll=True)
@@ -190,20 +189,10 @@
             give(chunk, i)
             return carry
 
-        lax.fori_loop(0, 16, at, 0)
-
-    def give_all(chunk):
-        def at(i, carry):
-            give(chunk, i)
-            return carry
-
-        lax.fori_loop(0, 16, at, 0)
-
-    def product_and_total(chunk, half):
-        product(chunk, half, chunk - 1)
+        lax.fori_loop(0, 16, at, 0, unroll=True)
 
     act = {
-        "S": spread, "A": arrive, "P": product, "C": combine, "U": fetched, "F": product_and_total, "G": give_all,
+        "S": spread, "A": arrive, "P": product, "C": combine, "U": fetched,
     }
     for name in ORDER:
         with scope("s_" + name):
@@ -251,7 +240,7 @@
             pltpu.SemaphoreType.DMA((CHUNKS,)),
             pltpu.SemaphoreType.DMA((CHUNKS, GROUPS)),
             pltpu.SemaphoreType.DMA,
-            pltpu.SemaphoreType.DMA((CHUNKS, HALVES)),
+            pltpu.SemaphoreType.DMA((CHUNKS, 4)),
             pltpu.SemaphoreType.DMA,
             pltpu.SemaphoreType.DMA,
         ],

time: 36 us -> 35.4 us (0.983)
  Pallas kernels: 35.3 us -> 34.6 us
    pallas_call x1, Pallas kernels: 35.3 us -> 34.6 us  [per_device(): pl.pallas_call(kernel, out_shape=pltpu.VMEM((2, 4, 128, 128), jnp.bfloat1...]
where the time goes in v4:
time: 35.4 us; the launch traced here: 35.3 us
  Pallas kernels  34.6 us (98%)
  local copies, waits for them, and re-layouts  0.71 us (2%)
    pallas_call x1, Pallas kernels, per_device(): pl.pallas_call(kernel, out_shape=pltpu.VMEM((2, 4, 128, 128), jnp.bfloat1...  34.6 us

profile of v4, /device:TPU:1, one launch (start us, length us, event | category | flops | bytes accessed | tf_op | source)
XLA Modules:
  0.0 35.3 jit_solution(17150447955159898387)
XLA Ops:
  0.0 34.6 %convolve.1 = bf16[2,4,128,128]{3,2,1,0:T(8,128)(2,1)S(1)} custom-call(bf16[2,512,128]{2,1,0:T(8,128)(2,1)} %bitcast.5, bf16[2,16,512,128]{3,2,1,0:T(8,128)(2,1)} %coupling.1, s32[16,16]{1,0:T(8,128)} %table_in.1), custom_call_target="tpu_custom_call" | custom-call | tf_op jit(solution)/shard_map/convolve/pallas_call | solution.py:219
  34.6 0.7 %copy.6 = bf16[2,4,1,1,128,128]{5,4,3,2,1,0:T(8,128)(2,1)} copy(bf16[2,4,1,1,128,128]{5,4,3,2,1,0:T(8,128)(2,1)S(1)} %bitcast.4) | data formatting | bytes 524288

commit v5 on v4

--- a/solution.py
+++ b/solution.py
@@ -14,7 +14,7 @@
 GROUPS = 8
 HALVES = 2
 NEAR_FIRST = (0, 1, 3, 2)
-X_STEPS = (0, 1, 3, 2)
+X_STEPS = (0, 2, 1, 3)
 FLIGHT = 1
 DEAL = ((0, range(16)), (1, range(16)))
 ORDER = (

time: 35.4 us -> 35.1 us (level)
  no operation moved by 1% of the time
where the time goes in v5:
time: 35.1 us; the launch traced here: 35 us
  Pallas kernels  34.3 us (98%)
  local copies, waits for them, and re-layouts  0.71 us (2%)
    pallas_call x1, Pallas kernels, per_device(): pl.pallas_call(kernel, out_shape=pltpu.VMEM((2, 4, 128, 128), jnp.bfloat1...  34.3 us
    unnamed x1, local copies, waits for them, and re-layouts  0.71 us

profile of v5, /device:TPU:1, one launch (start us, length us, event | category | flops | bytes accessed | tf_op | source)
XLA Modules:
  0.0 35.0 jit_solution(6713249321558532946)
XLA Ops:
  0.0 34.3 %convolve.1 = bf16[2,4,128,128]{3,2,1,0:T(8,128)(2,1)S(1)} custom-call(bf16[2,512,128]{2,1,0:T(8,128)(2,1)} %bitcast.5, bf16[2,16,512,128]{3,2,1,0:T(8,128)(2,1)} %coupling.1, s32[16,16]{1,0:T(8,128)} %table_in.1), custom_call_target="tpu_custom_call" | custom-call | tf_op jit(solution)/shard_map/convolve/pallas_call | solution.py:219
  34.3 0.7 %copy.6 = bf16[2,4,1,1,128,128]{5,4,3,2,1,0:T(8,128)(2,1)} copy(bf16[2,4,1,1,128,128]{5,4,3,2,1,0:T(8,128)(2,1)S(1)} %bitcast.4) | data formatting | bytes 524288

commit v6 on v5

--- a/solution.py
+++ b/solution.py
@@ -116,7 +116,7 @@
         block = green.at[chunk, x, pl.ds(group * per_group, per_group)]
         landed(block, in_recv.at[chunk, group])
         for x_step in X_STEPS[1:]:
-            send(block, block, x_send, x_recv.at[chunk, group * 4 // GROUPS], (z, (x + x_step) % 4, k)).start()
+            send(block, block, x_send, x_recv.at[chunk, group * 4 // GROUPS], (z, (x + x_step + 2 * core * (x_step % 2)) % 4, k)).start()
 
     def arrive(chunk, first, last):
         if first == 0:

time: 35.1 us -> 35 us (level)
  no operation moved by 1% of the time
where the time goes in v6:
time: 35 us; the launch traced here: 34.9 us
  Pallas kernels  34.2 us (98%)
  local copies, waits for them, and re-layouts  0.71 us (2%)
    pallas_call x1, Pallas kernels, per_device(): pl.pallas_call(kernel, out_shape=pltpu.VMEM((2, 4, 128, 128), jnp.bfloat1...  34.2 us
    unnamed x1, local copies, waits for them, and re-layouts  0.71 us

profile of v6, /device:TPU:1, one launch (start us, length us, event | category | flops | bytes accessed | tf_op | source)
XLA Modules:
  0.0 34.9 jit_solution(9794423690345675326)
XLA Ops:
  0.0 34.2 %convolve.1 = bf16[2,4,128,128]{3,2,1,0:T(8,128)(2,1)S(1)} custom-call(bf16[2,512,128]{2,1,0:T(8,128)(2,1)} %bitcast.5, bf16[2,16,512,128]{3,2,1,0:T(8,128)(2,1)} %coupling.1, s32[16,16]{1,0:T(8,128)} %table_in.1), custom_call_target="tpu_custom_call" | custom-call | tf_op jit(solution)/shard_map/convolve/pallas_call | solution.py:219
  34.2 0.7 %copy.6 = bf16[2,4,1,1,128,128]{5,4,3,2,1,0:T(8,128)(2,1)} copy(bf16[2,4,1,1,128,128]{5,4,3,2,1,0:T(8,128)(2,1)S(1)} %bitcast.4) | data formatting | bytes 524288

commit v7 on v5

--- a/solution.py
+++ b/solution.py
@@ -16,7 +16,7 @@
 NEAR_FIRST = (0, 1, 3, 2)
 X_STEPS = (0, 2, 1, 3)
 FLIGHT = 1
-DEAL = ((0, range(16)), (1, range(16)))
+DEAL = ((0, range(8, 16)), (0, range(8)), (1, range(16)))
 ORDER = (
     "S01", "S02", "S03", "S11", "S12", "S04", "S13", "S05", "S06", "S07", "A002", "U", "P002", "S14",
     "S15", "S16", "S17", "A102", "P102", "A023", "P023", "A034", "P034", "C0", "A123", "P123", "A134",

time: 35.1 us -> 35 us (level)
  no operation moved by 1% of the time
where the time goes in v7:
time: 35 us; the launch traced here: 34.9 us
  Pallas kernels  34.2 us (98%)
  local copies, waits for them, and re-layouts  0.71 us (2%)
    pallas_call x1, Pallas kernels, per_device(): pl.pallas_call(kernel, out_shape=pltpu.VMEM((2, 4, 128, 128), jnp.bfloat1...  34.2 us
    unnamed x1, local copies, waits for them, and re-layouts  0.71 us

profile of v7, /device:TPU:1, one launch (start us, length us, event | category | flops | bytes accessed | tf_op | source)
XLA Modules:
  0.0 34.9 jit_solution(324155214645683782)
XLA Ops:
  0.0 34.2 %convolve.1 = bf16[2,4,128,128]{3,2,1,0:T(8,128)(2,1)S(1)} custom-call(bf16[2,512,128]{2,1,0:T(8,128)(2,1)} %bitcast.5, bf16[2,16,512,128]{3,2,1,0:T(8,128)(2,1)} %coupling.1, s32[16,16]{1,0:T(8,128)} %table_in.1), custom_call_target="tpu_custom_call" | custom-call | tf_op jit(solution)/shard_map/convolve/pallas_call | solution.py:219
  34.2 0.7 %copy.6 = bf16[2,4,1,1,128,128]{5,4,3,2,1,0:T(8,128)(2,1)} copy(bf16[2,4,1,1,128,128]{5,4,3,2,1,0:T(8,128)(2,1)S(1)} %bitcast.4) | data formatting | bytes 524288
